TPU v7x, 32 devices: a whole 2x2x4 slice. The times are simulated.
32 devices in a mesh: parts: 2 (over y), mem: 4 (over z), space: 4 (over x, core).
Axes of the slice: x: 2, y: 2, z: 4, core: 2. Of those that a mesh axis runs over, the one named last changes fastest.
Arguments:
- ensemble: bfloat16 [64, 70, 8192], P('mem', None, ('parts', 'space')), parts along dimension 2, may hold values from -6 to 6
- transform: bfloat16 [128, 64], P('parts'), parts along dimension 0, may hold values from -0.75 to 0.75
- obs_operator: bfloat16 [16, 70], replicated, may hold values from -0.75 to 0.75
- obs_weight: float32 [16, 8192], P(None, ('parts', 'space')), parts along dimension 1, may hold values from 0.25 to 40, as said below
Outputs:
- analysis: bfloat16 [64, 70, 8192], P('mem', None, ('parts', 'space')), parts along dimension 2
- prior_gram: float32 [128, 64], P('parts'), parts along dimension 0
- posterior_gram: float32 [128, 64], P('parts'), parts along dimension 0
There are 2 independent parts, one for each index of `parts`. A program takes and returns all parts, laid end to end along the dimension named above; an argument that names none is the same for every part. Nothing has to cross between parts.
Inputs may be any that keep to these rules, and one draw needn't show every extreme that they name: `obs_weight`: positive.
All inputs are finite; a program needn't handle non-finite values.
Results may differ from a plain program's by a relative error of at most 0.001.
Values may be sent and summed in bfloat16 or wider, within the bound.
A program may use at most 64 MiB of HBM per device.

v0:
```python
import jax
import jax.numpy as jnp
from jax import lax
from jax.sharding import PartitionSpec as P

MEMBERS = 64
HIGHEST = lax.Precision.HIGHEST


def gram_terms(observed, weights):
    departures = observed - jnp.sum(observed, axis=0) / MEMBERS
    weighted = departures * weights[None, :, :]
    partial_gram = jnp.einsum("ioc,joc->ij", weighted, departures, precision=HIGHEST)
    return (partial_gram, jnp.sum(weights))


def per_device(ensemble, transform, obs_operator, obs_weight):
    local_members = ensemble.shape[0]
    mixing = transform.astype(jnp.float32)
    own_start = lax.axis_index("mem") * local_members
    own_columns = lax.dynamic_slice_in_dim(transform, own_start, local_members, 1)
    keep_mean = 1.0 - jnp.sum(own_columns.astype(jnp.float32), axis=0)
    members_block = lax.all_gather(ensemble, "mem", axis=0, tiled=True)
    combined = jnp.einsum(
        "kj,kvc->jvc", own_columns, members_block, preferred_element_type=jnp.float32
    )
    totals = jnp.sum(members_block, axis=0, dtype=jnp.float32)
    results = (totals, combined)
    totals = results[0]
    combined = results[1]
    member_mean = totals / MEMBERS
    analysis = (combined + member_mean[None, :, :] * keep_mean[:, None, None]).astype(jnp.bfloat16)
    observed = jnp.einsum("ov,mvc->moc", obs_operator, ensemble, preferred_element_type=jnp.float32)
    by_columns = lax.all_to_all(
        observed.astype(jnp.bfloat16), "mem", split_axis=2, concat_axis=0, tiled=True
    ).astype(observed.dtype)
    cells_here = by_columns.shape[2]
    own_weights = lax.dynamic_slice_in_dim(
        obs_weight, lax.axis_index("mem") * cells_here, cells_here, 1
    )
    partial_gram, weight_sum = gram_terms(by_columns, own_weights)
    gram_sum, weight_total = lax.psum((partial_gram, weight_sum), ("mem", "space"))
    prior_gram = gram_sum / weight_total
    carried = jnp.dot(mixing.T, prior_gram, precision=HIGHEST)
    posterior_gram = jnp.dot(carried, mixing, precision=HIGHEST)
    return (analysis, prior_gram, posterior_gram)


def solution(mesh):
    return jax.shard_map(
        per_device,
        mesh=mesh,
        in_specs=(
            P("mem", None, ("parts", "space")),
            P("parts", None),
            P(),
            P(None, ("parts", "space")),
        ),
        out_specs=(P("mem", None, ("parts", "space")), P("parts", None), P("parts", None)),
        check_vma=False,
    )
```

profile of v0, /device:TPU:0, one launch (start us, length us, event | category | flops | bytes accessed | tf_op | source)
XLA Modules:
  0.0 202.9 jit_solution(353153275937876548)
XLA Ops:
  7.2 0.0 copy-start
  7.2 0.0 all-gather.2.cloned.1.call-start
  7.2 0.7 all-gather.2.cloned.1.call-update
  7.9 3.0 %fusion.7 = bf16[16,16,1024]{2,1,0:T(8,128)(2,1)S(1)} fusion(bf16[16,70,1024]{2,0,1:T(8,128)(2,1)} %param.4, bf16[16,70]{1,0:T(8,128)(2,1)} %param.6), kind=kOutput, calls=%fused_computation.8 | convolution fusion | flops 36962304 | bytes 2820288 | tf_op jit(solution)/shard_map/ov,mvc->moc/dot_general | solution.py:33
  10.9 4.7 %copy.25 = bf16[16,16,1024]{1,0,2:T(8,128)(2,1)} copy(bf16[16,16,1024]{2,1,0:T(8,128)(2,1)S(1)} %fusion.7) | data formatting | bytes 1048576 | tf_op jit(solution)/shard_map/convert_element_type | solution.py:35
  15.6 6.6 %reshape.27 = bf16[4,2,32768]{2,1,0:T(2,128)(2,1)} reshape(bf16[1024,16,16]{2,1,0:T(8,128)(2,1)} %bitcast.28) | data formatting | bytes 1048576
  22.2 6.4 %all-to-all-start = ((bf16[4,2,32768]{2,1,0:T(2,128)(2,1)}), bf16[4,2,32768]{2,1,0:T(2,128)(2,1)S(1)}, u32[]{:S(2)}, u32[]{:S(2)}) async-start(bf16[4,2,32768]{2,1,0:T(2,128)(2,1)} %reshape.27), calls=%async_computation | async-start | bytes 1048576 | tf_op jit(solution)/shard_map/all_to_all | solution.py:34
  28.6 0.0 copy-done
  28.6 0.1 constant_dynamic-slice_fusion.1
  28.7 0.1 copy.28
  28.8 0.1 convert_reduce_fusion.2
  28.9 1.3 fusion.16
  30.2 25.9 %all-to-all-done = bf16[4,2,32768]{2,1,0:T(2,128)(2,1)S(1)} async-done(((bf16[4,2,32768]{2,1,0:T(2,128)(2,1)}), bf16[4,2,32768]{2,1,0:T(2,128)(2,1)S(1)}, u32[]{:S(2)}, u32[]{:S(2)}) %all-to-all-start) | async-done | bytes 524320 | tf_op jit(solution)/shard_map/all_to_all | solution.py:34
  56.1 4.1 %reshape.28 = bf16[1024,16,16]{2,1,0:T(8,128)(2,1)} reshape(bf16[4,2,32768]{2,1,0:T(2,128)(2,1)S(1)} %all-to-all-done) | data formatting | bytes 1048576
  60.2 6.1 %bitcast_convert_fusion = f32[16,16,1024]{1,0,2:T(8,128)} fusion(bf16[1024,16,16]{2,1,0:T(8,128)(2,1)} %reshape.28), kind=kLoop, calls=%fused_computation.22 | loop fusion | flops 262144 | bytes 1572864 | tf_op jit(solution)/shard_map/convert_element_type | solution.py:36
  66.4 6.6 %copy.26 = f32[4,16,16,256]{3,1,0,2:T(8,128)S(1)} copy(f32[4,16,16,256]{2,1,3,0:T(8,128)} %bitcast.27) | data formatting | bytes 2097152 | tf_op jit(solution)/shard_map/convert_element_type | solution.py:36
  72.9 4.2 %convert_reduce_fusion.1 = f32[16,1024]{0,1:T(8,128)S(1)} fusion(bf16[1024,16,16]{2,1,0:T(8,128)(2,1)} %reshape.28), kind=kLoop, calls=%fused_computation.4 | loop fusion | flops 507904 | bytes 589824 | tf_op jit(solution)/shard_map/reduce_sum | solution.py:11
  77.2 0.1 copy.27
  77.3 0.1 bitcast_subtract_fusion
  77.5 1.0 fusion.10
  78.5 63.8 %all-reduce = (f32[64,64]{1,0:T(8,128)S(1)}, f32[]{:T(128)}) all-reduce(f32[64,64]{1,0:T(8,128)S(1)} %fusion.10, f32[]{:T(128)} %get-tuple-element.5), channel_id=1, replica_groups=mesh['parts'=2,'mem'=4,'space'=4] {'mem','space'}, use_global_device_ids=true, to_apply=%region_4.0 | all-reduce | flops 4097 | bytes 32776 | tf_op jit(solution)/shard_map/psum | solution.py:42
  142.3 0.7 broadcast_divide_fusion
  142.9 0.0 copy-start.2
  142.9 0.2 fusion.17
  143.2 0.8 fusion.18
  144.0 42.6 %all-gather.2.cloned.1.call-done = bf16[64,70,1024]{2,0,1:T(8,128)(2,1)} async-done(((bf16[16,70,1024]{2,0,1:T(8,128)(2,1)}), bf16[64,70,1024]{2,0,1:T(8,128)(2,1)}) %all-gather.2.cloned.1.call-update) | async-done | bytes 9175056 | tf_op jit(solution)/shard_map/all_gather | solution.py:23
  186.6 0.0 copy-start.1
  186.6 6.7 %convert_reduce_fusion = f32[70,1024]{1,0:T(8,128)S(1)} fusion(bf16[64,70,1024]{2,0,1:T(8,128)(2,1)} %all-gather.2.cloned.1.call-done), kind=kLoop, calls=%fused_computation | loop fusion | flops 9103360 | bytes 9461760 | tf_op jit(solution)/shard_map/reduce_sum | solution.py:27
  193.3 0.0 copy-done.2
  193.3 0.0 copy-done.1
  193.3 2.8 %add_convert_fusion = bf16[16,70,1024]{2,0,1:T(8,128)(2,1)} fusion(f32[16]{0:T(128)S(1)} %broadcast_subtract_fusion, f32[70,1024]{1,0:T(8,128)S(1)} %broadcast_multiply_fusion, bf16[64,70,1024]{2,0,1:T(8,128)(2,1)S(1)} %copy-done.1, bf16[64,16]{1,0:T(8,128)(2,1)S(1)} %constant_dynamic-slice_fusion.1), kind=kOutput, calls=%fused_computation.1 | convolution fusion | flops 150241280 | bytes 11757632 | tf_op jit(solution)/shard_map/kj,kvc->jvc/dot_general | solution.py:24
  (4 shorter events, 0.1 us)
Async XLA Ops:
  7.2 21.4 %copy-start = (bf16[64,64]{1,0:T(8,128)(2,1)S(1)}, bf16[64,64]{1,0:T(8,128)(2,1)}, u32[]{:S(2)}) copy-start(bf16[64,64]{1,0:T(8,128)(2,1)} %param.5) | copy-start | bytes 24580
  7.2 179.4 %all-gather.2.cloned.1.call-start = ((), (), s32[]{:S(2)}) async-start(), calls=%async_computation.1 | async-start | bytes 11468800 | tf_op jit(solution)/shard_map/all_gather | solution.py:23
  22.2 33.9 %all-to-all-start = ((bf16[4,2,32768]{2,1,0:T(2,128)(2,1)}), bf16[4,2,32768]{2,1,0:T(2,128)(2,1)S(1)}, u32[]{:S(2)}, u32[]{:S(2)}) async-start(bf16[4,2,32768]{2,1,0:T(2,128)(2,1)} %reshape.27), calls=%async_computation | async-start | bytes 1048576 | tf_op jit(solution)/shard_map/all_to_all | solution.py:34
  142.9 50.3 %copy-start.2 = (f32[64,64]{1,0:T(8,128)}, f32[64,64]{1,0:T(8,128)S(1)}, u32[]{:S(2)}) copy-start(f32[64,64]{1,0:T(8,128)S(1)} %broadcast_divide_fusion) | copy-start | bytes 49156
  186.6 6.7 %copy-start.1 = (bf16[64,70,1024]{2,0,1:T(8,128)(2,1)S(1)}, bf16[64,70,1024]{2,0,1:T(8,128)(2,1)}, u32[]{:S(2)}) copy-start(bf16[64,70,1024]{2,0,1:T(8,128)(2,1)} %all-gather.2.cloned.1.call-done) | copy-start | bytes 27525124
Sparse Core Ops, SparseCore 0:
  9.6 176.9 all-gather.1
where the time goes:
time: 203 us
  waiting for transfers between devices  69.2 us (34%)
  blocking collectives  63.8 us (31%)
  local copies, waits for them, and re-layouts  22.2 us (11%)
  other arithmetic  19.3 us (10%)
  between operations  14.1 us (7%)
  matrix products  7.83 us (4%)
  starting transfers between devices  6.41 us (3%)
    psum x1, blocking collectives, per_device(): lax.psum((partial_gram, weight_sum), ('mem', 'space'))  63.8 us
    all_gather x1, waiting for transfers between devices, per_device(): members_block = lax.all_gather(ensemble, 'mem', axis=0, tiled=True)  42.6 us
    all_to_all x1, waiting for transfers between devices, per_device(): lax.all_to_all(observed.astype(jnp.bfloat16), 'mem', split_axis=2, concat...  25.9 us
    unnamed x9, local copies, waits for them, and re-layouts  10.8 us
    reduce_sum x1, other arithmetic, per_device(): totals = jnp.sum(members_block, axis=0, dtype=jnp.float32)  6.65 us
    convert_element_type x1, local copies, waits for them, and re-layouts, per_device(): by_columns = lax.all_to_all(observed.astype(jnp.bfloat16), 'mem', split_a...  6.59 us
    all_to_all x1, starting transfers between devices, per_device(): lax.all_to_all(observed.astype(jnp.bfloat16), 'mem', split_axis=2, concat...  6.38 us
    convert_element_type x1, other arithmetic, per_device(): by_columns = lax.all_to_all(observed.astype(jnp.bfloat16), 'mem', split_a...  6.11 us
  transfers between devices with their start and end apart: 2, of which 2 were waited for; matrix products, arithmetic and copies ran while one was open for 20% of the time, Pallas kernels for 0%

commit v1 on v0

--- a/solution.py
+++ b/solution.py
@@ -5,6 +5,16 @@
 
 MEMBERS = 64
 HIGHEST = lax.Precision.HIGHEST
+
+
+def turned_line(x, name, along):
+    count = lax.axis_size(name)
+    held, blocks = (x, [x])
+    for _ in range(count - 1):
+        held = lax.ppermute(held, name, [(i, (i + 1) % count) for i in range(count)])
+        blocks.insert(0, held)
+    flat = jnp.concatenate(blocks, axis=along)
+    return jnp.roll(flat, (lax.axis_index(name) + 1) * x.shape[along], axis=along)
 
 
 def gram_terms(observed, weights):
@@ -20,7 +30,7 @@
     own_start = lax.axis_index("mem") * local_members
     own_columns = lax.dynamic_slice_in_dim(transform, own_start, local_members, 1)
     keep_mean = 1.0 - jnp.sum(own_columns.astype(jnp.float32), axis=0)
-    members_block = lax.all_gather(ensemble, "mem", axis=0, tiled=True)
+    members_block = turned_line(ensemble, "mem", 0)
     combined = jnp.einsum(
         "kj,kvc->jvc", own_columns, members_block, preferred_element_type=jnp.float32
     )

time: 203 us -> 285 us (1.40)
  waiting for transfers between devices: 69.2 us -> 144 us
  local copies, waits for them, and re-layouts: 22.2 us -> 41.9 us
  between operations: 14.1 us -> 0.74 us
  blocking collectives: 63.8 us -> 58.9 us
  matrix products: 7.83 us -> 12.3 us
    ppermute x0 -> x3, waiting for transfers between devices: none -> 87.2 us  [turned_line(): lax.ppermute(held, name, [(i, (i + 1) % count) for i in range(count)])]
    all_gather x1 -> x0, waiting for transfers between devices: 42.6 us -> none  [per_device(): members_block = lax.all_gather(ensemble, 'mem', axis=0, tiled=True)]
    all_to_all x1, waiting for transfers between devices: 25.9 us -> 57.2 us  [per_device(): lax.all_to_all(observed.astype(jnp.bfloat16), 'mem', split_axis=2, concat...]
    unnamed x9 -> x20, local copies, waits for them, and re-layouts: 10.8 us -> 28.9 us
    psum x1, blocking collectives: 63.8 us -> 58.9 us  [per_device(): lax.psum((partial_gram, weight_sum), ('mem', 'space'))]
    dot_general x1, matrix products: 2.79 us -> 6.43 us  [per_device(): jnp.einsum('kj,kvc->jvc', own_columns, members_block, preferred_element_t...]
    ppermute x0 -> x3, starting transfers between devices: none -> 3.11 us  [turned_line(): lax.ppermute(held, name, [(i, (i + 1) % count) for i in range(count)])]
  transfers between devices with their start and end apart: 2 -> 4, of which waited for: 2 -> 3; matrix products, arithmetic and copies ran while one was open for 20% -> 14% of each run, Pallas kernels for 0% -> 0%
where the time goes in v1:
time: 285 us
  waiting for transfers between devices  144 us (51%)
  blocking collectives  58.9 us (21%)
  local copies, waits for them, and re-layouts  41.9 us (15%)
  other arithmetic  19.2 us (7%)
  matrix products  12.3 us (4%)
  starting transfers between devices  7.36 us (3%)
    ppermute x3, waiting for transfers between devices, turned_line(): lax.ppermute(held, name, [(i, (i + 1) % count) for i in range(count)])  87.2 us
    psum x1, blocking collectives, per_device(): lax.psum((partial_gram, weight_sum), ('mem', 'space'))  58.9 us
    all_to_all x1, waiting for transfers between devices, per_device(): lax.all_to_all(observed.astype(jnp.bfloat16), 'mem', split_axis=2, concat...  57.2 us
    unnamed x20, local copies, waits for them, and re-layouts  28.9 us
    convert_element_type x1, local copies, waits for them, and re-layouts, per_device(): by_columns = lax.all_to_all(observed.astype(jnp.bfloat16), 'mem', split_a...  6.53 us
    reduce_sum x1, other arithmetic, per_device(): totals = jnp.sum(members_block, axis=0, dtype=jnp.float32)  6.43 us
    dot_general x1, matrix products, per_device(): jnp.einsum('kj,kvc->jvc', own_columns, members_block, preferred_element_t...  6.43 us
    convert_element_type x1, other arithmetic, per_device(): by_columns = lax.all_to_all(observed.astype(jnp.bfloat16), 'mem', split_a...  6.07 us
  transfers between devices with their start and end apart: 4, of which 3 were waited for; matrix products, arithmetic and copies ran while one was open for 14% of the time, Pallas kernels for 0%

profile of v1, /device:TPU:0, one launch (start us, length us, event | category | flops | bytes accessed | tf_op | source)
XLA Modules:
  0.0 284.7 jit_solution(1606655496220426348)
XLA Ops:
  0.6 3.1 %collective-permute-start = (bf16[16,70,1024]{2,0,1:T(8,128)(2,1)}, bf16[16,70,1024]{2,0,1:T(8,128)(2,1)S(1)}, u32[]{:S(2)}, u32[]{:S(2)}) collective-permute-start(bf16[16,70,1024]{2,0,1:T(8,128)(2,1)} %param.4), channel_id=1, source_target_pairs={{0,4},{4,8},{8,12},{12,0},{1,5},{5,9},{9,13},{13,1},{2,6},{6,10},{... | collective-permute-start | bytes 6881288 | tf_op jit(solution)/shard_map/ppermute | solution.py:14
  3.8 52.1 %collective-permute-done = bf16[16,70,1024]{2,0,1:T(8,128)(2,1)S(1)} collective-permute-done((bf16[16,70,1024]{2,0,1:T(8,128)(2,1)}, bf16[16,70,1024]{2,0,1:T(8,128)(2,1)S(1)}, u32[]{:S(2)}, u32[]{:S(2)}) %collective-permute-start) | collective-permute-done | bytes 2293792 | tf_op jit(solution)/shard_map/ppermute | solution.py:14
  55.8 3.8 %fusion.11 = bf16[16,16,1024]{2,1,0:T(8,128)(2,1)S(1)} fusion(bf16[16,70,1024]{2,0,1:T(8,128)(2,1)} %param.4, bf16[16,70]{1,0:T(8,128)(2,1)} %param.6), kind=kOutput, calls=%fused_computation.10 | convolution fusion | flops 36962304 | bytes 2820288 | tf_op jit(solution)/shard_map/ov,mvc->moc/dot_general | solution.py:43
  59.7 4.7 %copy.25 = bf16[16,16,1024]{1,0,2:T(8,128)(2,1)} copy(bf16[16,16,1024]{2,1,0:T(8,128)(2,1)S(1)} %fusion.11) | data formatting | bytes 1048576 | tf_op jit(solution)/shard_map/convert_element_type | solution.py:45
  64.4 6.5 %reshape.27 = bf16[4,2,32768]{2,1,0:T(2,128)(2,1)} reshape(bf16[1024,16,16]{2,1,0:T(8,128)(2,1)} %bitcast.27) | data formatting | bytes 1048576
  70.8 4.3 %all-to-all-start = ((bf16[4,2,32768]{2,1,0:T(2,128)(2,1)}), bf16[4,2,32768]{2,1,0:T(2,128)(2,1)S(1)}, u32[]{:S(2)}, u32[]{:S(2)}) async-start(bf16[4,2,32768]{2,1,0:T(2,128)(2,1)} %reshape.27), calls=%async_computation | async-start | bytes 1048576 | tf_op jit(solution)/shard_map/all_to_all | solution.py:44
  75.1 0.1 constant_dynamic-slice_fusion.1
  75.2 0.1 copy.28
  75.3 0.1 convert_reduce_fusion.2
  75.4 35.1 %collective-permute-done.1 = bf16[16,70,1024]{2,0,1:T(8,128)(2,1)} collective-permute-done((bf16[16,70,1024]{2,0,1:T(8,128)(2,1)S(1)}, bf16[16,70,1024]{2,0,1:T(8,128)(2,1)}, u32[]{:S(2)}, u32[]{:S(2)}) %collective-permute-start.1) | collective-permute-done | bytes 2293792 | tf_op jit(solution)/shard_map/ppermute | solution.py:14
  110.5 1.3 fusion.21
  111.8 57.2 %all-to-all-done = bf16[4,2,32768]{2,1,0:T(2,128)(2,1)S(1)} async-done(((bf16[4,2,32768]{2,1,0:T(2,128)(2,1)}), bf16[4,2,32768]{2,1,0:T(2,128)(2,1)S(1)}, u32[]{:S(2)}, u32[]{:S(2)}) %all-to-all-start) | async-done | bytes 524320 | tf_op jit(solution)/shard_map/all_to_all | solution.py:44
  169.0 4.1 %reshape.28 = bf16[1024,16,16]{2,1,0:T(8,128)(2,1)} reshape(bf16[4,2,32768]{2,1,0:T(2,128)(2,1)S(1)} %all-to-all-done) | data formatting | bytes 1048576
  173.2 6.1 %bitcast_convert_fusion = f32[16,16,1024]{1,0,2:T(8,128)} fusion(bf16[1024,16,16]{2,1,0:T(8,128)(2,1)} %reshape.28), kind=kLoop, calls=%fused_computation.33 | loop fusion | flops 262144 | bytes 1572864 | tf_op jit(solution)/shard_map/convert_element_type | solution.py:46
  179.3 6.5 %copy.26 = f32[4,16,16,256]{3,1,0,2:T(8,128)S(1)} copy(f32[4,16,16,256]{2,1,3,0:T(8,128)} %bitcast.26) | data formatting | bytes 2097152 | tf_op jit(solution)/shard_map/convert_element_type | solution.py:46
  185.8 4.2 %convert_reduce_fusion.1 = f32[16,1024]{0,1:T(8,128)S(1)} fusion(bf16[1024,16,16]{2,1,0:T(8,128)(2,1)} %reshape.28), kind=kLoop, calls=%fused_computation.6 | loop fusion | flops 507904 | bytes 589824 | tf_op jit(solution)/shard_map/reduce_sum | solution.py:21
  190.1 0.1 bitcast_subtract_fusion
  190.3 1.0 fusion.14
  191.3 58.9 %all-reduce = (f32[64,64]{1,0:T(8,128)S(1)}, f32[]{:T(128)}) all-reduce(f32[64,64]{1,0:T(8,128)S(1)} %fusion.14, f32[]{:T(128)} %get-tuple-element.5), channel_id=1, replica_groups=mesh['parts'=2,'mem'=4,'space'=4] {'mem','space'}, use_global_device_ids=true, to_apply=%region_4.5 | all-reduce | flops 4097 | bytes 32776 | tf_op jit(solution)/shard_map/psum | solution.py:52
  250.2 0.8 broadcast_divide_fusion
  251.0 0.2 fusion.22
  251.2 0.8 fusion.23
  252.1 3.3 %constant_dynamic-update-slice_fusion.7 = bf16[128,70,1024]{2,0,1:T(8,128)(2,1)} fusion(bf16[16,70,1024]{2,0,1:T(8,128)(2,1)} %collective-permute-done.2), kind=kLoop, calls=%fused_computation.22 | loop fusion | bytes 4587520
  255.4 3.4 %constant_dynamic-update-slice_fusion.6 = bf16[128,70,1024]{2,0,1:T(8,128)(2,1)} fusion(bf16[128,70,1024]{2,0,1:T(8,128)(2,1)} %constant_dynamic-update-slice_fusion.7, bf16[16,70,1024]{2,0,1:T(8,128)(2,1)} %collective-permute-done.1), kind=kLoop, calls=%fused_computation.21 | loop fusion | bytes 4587520
  258.8 1.6 constant_dynamic-update-slice_fusion.5
  260.4 1.5 constant_dynamic-update-slice_fusion.4
  262.0 3.3 %constant_dynamic-update-slice_fusion.3 = bf16[128,70,1024]{2,0,1:T(8,128)(2,1)} fusion(bf16[128,70,1024]{2,0,1:T(8,128)(2,1)} %constant_dynamic-update-slice_fusion.4, bf16[16,70,1024]{2,0,1:T(8,128)(2,1)} %collective-permute-done.2), kind=kLoop, calls=%fused_computation.18 | loop fusion | bytes 4587520
  265.3 3.3 %constant_dynamic-update-slice_fusion.2 = bf16[128,70,1024]{2,0,1:T(8,128)(2,1)} fusion(bf16[128,70,1024]{2,0,1:T(8,128)(2,1)} %constant_dynamic-update-slice_fusion.3, bf16[16,70,1024]{2,0,1:T(8,128)(2,1)} %collective-permute-done.1), kind=kLoop, calls=%fused_computation.17 | loop fusion | bytes 4587520
  268.6 1.6 constant_dynamic-update-slice_fusion.1
  270.3 1.6 constant_dynamic-update-slice_fusion
  271.8 6.4 %convert_reduce_fusion = f32[70,1024]{1,0:T(8,128)S(1)} fusion(bf16[128,70,1024]{2,0,1:T(8,128)(2,1)} %constant_dynamic-update-slice_fusion, s32[]{:T(128)S(6)} %select_n.21), kind=kLoop, calls=%fused_computation | loop fusion | flops 9103360 | bytes 9461764 | tf_op jit(solution)/shard_map/reduce_sum | solution.py:37
  278.3 6.4 %add_convert_fusion = bf16[16,70,1024]{2,0,1:T(8,128)(2,1)} fusion(f32[16]{0:T(128)S(1)} %broadcast_subtract_fusion, f32[70,1024]{1,0:T(8,128)S(1)} %broadcast_multiply_fusion, bf16[128,70,1024]{2,0,1:T(8,128)(2,1)} %constant_dynamic-update-slice_fusion, s32[]{:T(128)S(6)} %select_n.21, bf16[64,16]{1,0:T(8,128)(2,1)S(1)} %constant_dynamic-slice_fusion.1), kind=kOutput, calls=%fused_computation.3 | convolution fusion | flops 150241280 | bytes 11757636 | tf_op jit(solution)/shard_map/kj,kvc->jvc/dot_general | solution.py:34
  (18 shorter events, 0.2 us)
Async XLA Ops:
  0.6 74.5 %copy-start = (bf16[64,64]{1,0:T(8,128)(2,1)S(1)}, bf16[64,64]{1,0:T(8,128)(2,1)}, u32[]{:S(2)}) copy-start(bf16[64,64]{1,0:T(8,128)(2,1)} %param.5) | copy-start | bytes 24580
  0.6 55.2 %collective-permute-start = (bf16[16,70,1024]{2,0,1:T(8,128)(2,1)}, bf16[16,70,1024]{2,0,1:T(8,128)(2,1)S(1)}, u32[]{:S(2)}, u32[]{:S(2)}) collective-permute-start(bf16[16,70,1024]{2,0,1:T(8,128)(2,1)} %param.4), channel_id=1, source_target_pairs={{0,4},{4,8},{8,12},{12,0},{1,5},{5,9},{9,13},{13,1},{2,6},{6,10},{... | collective-permute-start | bytes 6881288 | tf_op jit(solution)/shard_map/ppermute | solution.py:14
  55.8 123.4 %copy-start.2 = (bf16[16,70,1024]{2,0,1:T(8,128)(2,1)}, bf16[16,70,1024]{2,0,1:T(8,128)(2,1)S(1)}, u32[]{:S(2)}) copy-start(bf16[16,70,1024]{2,0,1:T(8,128)(2,1)S(1)} %collective-permute-done) | copy-start | bytes 6881284
  55.8 54.7 %collective-permute-start.1 = (bf16[16,70,1024]{2,0,1:T(8,128)(2,1)S(1)}, bf16[16,70,1024]{2,0,1:T(8,128)(2,1)}, u32[]{:S(2)}, u32[]{:S(2)}) collective-permute-start(bf16[16,70,1024]{2,0,1:T(8,128)(2,1)S(1)} %collective-permute-done), channel_id=1, source_target_pairs={{0,4},{4,8},{8,12},{12,0},{1,5},{5,9},{9,13},{13,1},{2,6},{6,10},{... | collective-permute-start | bytes 6881288 | tf_op jit(solution)/shard_map/ppermute | solution.py:14
  70.8 98.2 %all-to-all-start = ((bf16[4,2,32768]{2,1,0:T(2,128)(2,1)}), bf16[4,2,32768]{2,1,0:T(2,128)(2,1)S(1)}, u32[]{:S(2)}, u32[]{:S(2)}) async-start(bf16[4,2,32768]{2,1,0:T(2,128)(2,1)} %reshape.27), calls=%async_computation | async-start | bytes 1048576 | tf_op jit(solution)/shard_map/all_to_all | solution.py:44
  110.5 141.6 %collective-permute-start.2 = (bf16[16,70,1024]{2,0,1:T(8,128)(2,1)}, bf16[16,70,1024]{2,0,1:T(8,128)(2,1)}, u32[]{:S(2)}, u32[]{:S(2)}) collective-permute-start(bf16[16,70,1024]{2,0,1:T(8,128)(2,1)} %collective-permute-done.1), channel_id=1, source_target_pairs={{0,4},{4,8},{8,12},{12,0},{1,5},{5,9},{9,13},{13,1},{2,6},{6,10},{... | collective-permute-start | bytes 6881288 | tf_op jit(solution)/shard_map/ppermute | solution.py:14
  190.1 70.3 %copy-start.1 = (bf16[16,70,1024]{2,0,1:T(8,128)(2,1)S(1)}, bf16[16,70,1024]{2,0,1:T(8,128)(2,1)}, u32[]{:S(2)}) copy-start(bf16[16,70,1024]{2,0,1:T(8,128)(2,1)} %param.4) | copy-start | bytes 6881284
  250.2 8.6 %copy-start.3 = (bf16[16,70,1024]{2,0,1:T(8,128)(2,1)S(1)}, bf16[16,70,1024]{2,0,1:T(8,128)(2,1)}, u32[]{:S(2)}) copy-start(bf16[16,70,1024]{2,0,1:T(8,128)(2,1)} %copy-done.2) | copy-start | bytes 6881284
  251.0 11.0 %copy-start.4 = (f32[64,64]{1,0:T(8,128)}, f32[64,64]{1,0:T(8,128)S(1)}, u32[]{:S(2)}) copy-start(f32[64,64]{1,0:T(8,128)S(1)} %broadcast_divide_fusion) | copy-start | bytes 49156
